TPU v7x, 512 devices: a whole 4x8x8 slice. The times are simulated.
512 devices in a mesh: elem: 128 (over z, x_lo, y), chan: 4 (over x_hi, core).
Axes of the slice: x: 4 (x_hi: 2, x_lo: 2; x = x_hi * 2 + x_lo), y: 8, z: 8, core: 2. Of those that a mesh axis runs over, the one named last changes fastest.
Arguments:
- voltages: bfloat16 [2, 16384, 19584], P(None, ('elem', 'chan')), may hold values from -6 to 6
- delays: int32 [16384], P(('elem', 'chan')), may hold values from 0 to 127
- prototype: bfloat16 [16, 1024], replicated, may hold values from -1.5 to 1.5
- subband_map: int32 [16], replicated, may hold values from 0 to 1023, as said below
- beam_weights: bfloat16 [512, 2, 16, 16384], P('elem', None, 'chan'), may hold values from -0.1875 to 0.1875
Outputs:
- element_power: bfloat16 [16384, 1024], P(('elem', 'chan'))
- beam_voltages: float32 [2, 64, 512], P(None, 'chan', 'elem')
Inputs may be any that keep to these rules, and one draw needn't show every extreme that they name: `subband_map`: distinct channel numbers.
All inputs are finite; a program needn't handle non-finite values.
Results may differ from a plain program's by a relative error of at most 0.007.
Values may be sent and summed in bfloat16 or wider, within the bound.
A program may use at most 128 MiB of HBM per device.

v0:
```python
import math
import jax
import jax.numpy as jnp
from jax import lax
from jax.sharding import Mesh
from jax.sharding import PartitionSpec as P

FRAMES = 4
SUB_C = 4
ELEM = ("elem_0", "elem_1", "elem_2")
ELEM_CHAN = ("elem_0", "elem_1", "elem_2", "chan")


def in_order(parts, dim):
    parts = jnp.moveaxis(parts, 0, dim)
    dims = parts.shape
    return parts.reshape(*dims[:dim], dims[dim] * dims[dim + 1], *dims[dim + 2 :])


def all_blocks(array, axes, turns):
    parts = array[None]
    for k in turns:
        parts = lax.all_gather(parts, axes[k], axis=0, tiled=True)
    held = [lax.axis_size(axes[k]) for k in reversed(turns)]
    parts = parts.reshape(*held, *array.shape)
    turned = sorted(range(len(turns)), key=lambda place: turns[len(turns) - 1 - place])
    return parts.transpose(*turned, *range(len(turns), parts.ndim)).reshape(-1, *array.shape)


def gather_axes(array, axes, turns, dim):
    return in_order(all_blocks(array, axes, turns), dim)


def filtered(voltages, delays, prototype):
    tap_count, chan_count = prototype.shape
    blocks = FRAMES + tap_count - 1
    window_len = blocks * chan_count

    def window(samples, offset):
        return lax.dynamic_slice_in_dim(samples, offset, window_len, 0)

    segments = jax.vmap(jax.vmap(window, in_axes=(0, 0)), in_axes=(0, None))(voltages, delays)
    segments = segments.reshape(voltages.shape[0], voltages.shape[1], blocks, chan_count)
    coeffs = prototype.astype(jnp.float32)
    running = jnp.zeros((voltages.shape[0], voltages.shape[1], FRAMES, chan_count), jnp.float32)
    for tap_index in range(tap_count):
        running = running + coeffs[tap_index] * segments[
            :, :, tap_index : tap_index + FRAMES, :
        ].astype(jnp.float32)
    return running.astype(jnp.bfloat16)


def spectra(filtered_wave):
    part_count, elem_count, frame_count, chan_count = filtered_wave.shape
    counter = jnp.arange(chan_count, dtype=jnp.int32)
    residue = counter[:, None] * counter[None, :] % chan_count
    radians = residue.astype(jnp.float32) * (2.0 * math.pi / chan_count)
    factor = 1.0 / math.sqrt(chan_count)
    basis = jnp.concatenate([jnp.cos(radians) * factor, jnp.sin(radians) * factor], axis=1)
    basis_high = basis.astype(jnp.bfloat16)
    basis_low = (basis - basis_high.astype(jnp.float32)).astype(jnp.bfloat16)
    flattened = filtered_wave.reshape(part_count * elem_count * frame_count, chan_count)
    product = jnp.dot(flattened, basis_high, preferred_element_type=jnp.float32)
    product = product + jnp.dot(flattened, basis_low, preferred_element_type=jnp.float32)
    product = product.reshape(part_count, elem_count, frame_count, 2, chan_count)
    spec_real = product[0, :, :, 0] + product[1, :, :, 1]
    spec_imag = product[1, :, :, 0] - product[0, :, :, 1]
    return (spec_real, spec_imag)


def beam_terms(spectra_part, weight_part):
    weight_real = weight_part[:, 0]
    weight_imag = weight_part[:, 1]

    def contract(spectral, weighting):
        return jnp.einsum("sfe,bse->sfb", spectral, weighting, preferred_element_type=jnp.float32)

    out_real = contract(spectra_part[0], weight_real) - contract(spectra_part[1], weight_imag)
    out_imag = contract(spectra_part[1], weight_real) + contract(spectra_part[0], weight_imag)
    return jnp.stack([out_real, out_imag])


def on_device(voltages, delays, prototype, subband_map, beam_weights):
    filtered_wave = filtered(voltages, delays, prototype)
    spec_real, spec_imag = spectra(filtered_wave)
    element_power = jnp.mean(spec_real * spec_real + spec_imag * spec_imag, axis=1).astype(
        jnp.bfloat16
    )
    picked = jnp.stack([spec_real[:, :, subband_map], spec_imag[:, :, subband_map]]).astype(
        jnp.bfloat16
    )
    picked = jnp.transpose(picked, (0, 3, 2, 1))
    turned = lax.all_to_all(picked, "chan", split_axis=1, concat_axis=3, tiled=True)
    local_beams = beam_weights.shape[0]
    summed = beam_terms(gather_axes(turned, ELEM, (1, 0, 2), 3), beam_weights)
    beam_voltages = summed.reshape(2, SUB_C * FRAMES, local_beams)
    return (element_power, beam_voltages)


def solution(mesh):
    finer = Mesh(
        mesh.devices.reshape(8, 2, 8, mesh.shape["chan"]), ("elem_0", "elem_1", "elem_2", "chan")
    )
    placed = (P(None, ELEM_CHAN, None), P(ELEM_CHAN), P(), P(), P(ELEM, None, "chan", None))
    return jax.shard_map(
        on_device,
        mesh=finer,
        in_specs=placed,
        out_specs=(P(ELEM_CHAN, None), P(None, "chan", ELEM)),
        check_vma=False,
    )
```

profile of v0, /device:TPU:2, one launch (start us, length us, event | category | flops | bytes accessed | tf_op | source)
XLA Modules:
  0.0 262.3 jit_solution(16402044286607184922)
XLA Ops:
  7.2 17.8 %sine_multiply_fusion = (f32[1024,1024]{1,0:T(8,128)}, f32[1024,1024]{1,0:T(8,128)}) fusion(), kind=kLoop, calls=%fused_computation.14 | loop fusion | flops 16777216 | bytes 8388608 | tf_op jit(solution)/shard_map/mul | solution.py:59
  27.1 88.3 %while.1 = (s32[]{:T(128)}, bf16[2,32,19584]{2,0,1:T(2,128)(2,1)S(1)}, s32[32,2]{0,1:T(2,128)S(1)}, bf16[32,2,19456]{2,1,0:T(2,128)(2,1)}, s32[]{:T(128)}) while((s32[]{:T(128)}, bf16[2,32,19584]{2,0,1:T(2,128)(2,1)S(1)}, s32[32,2]{0,1:T(2,128)S(1)}, bf16[32,2,19456]{2,1,0:T(2,128)(2,1)}, s32[]{:T(128)}) %tuple.51), condition=%wide.while_cond, body=%wide.while_body.sunk | while | flops 2 | bytes 157281 | solution.py:40
  38.8 2.1 bitcast_dynamic-update-slice_fusion.2
  44.3 2.1 bitcast_dynamic-update-slice_fusion.2
  47.1 2.1 bitcast_dynamic-update-slice_fusion.2
  88.4 2.1 bitcast_dynamic-update-slice_fusion.2
  107.7 2.1 bitcast_dynamic-update-slice_fusion.2
  113.2 2.1 bitcast_dynamic-update-slice_fusion.2
  115.3 3.6 %copy.41 = bf16[2,32,19456]{2,1,0:T(8,128)(2,1)} copy(bf16[2,32,19456]{2,0,1:T(2,128)(2,1)} %bitcast.82) | data formatting | bytes 4980736 | tf_op jit(solution)/shard_map/vmap(vmap())/gather | solution.py:40
  119.0 3.3 %reshape.48 = bf16[2,32,19,1024]{3,2,1,0:T(8,128)(2,1)S(1)} reshape(bf16[2,32,19456]{2,1,0:T(8,128)(2,1)} %copy.41) | data formatting | bytes 4980736 | tf_op jit(solution)/shard_map/reshape | solution.py:43
  122.3 5.1 %add_convert_fusion = bf16[2,32,4,1024]{3,2,1,0:T(4,128)(2,1)} fusion(bf16[2,32,19,1024]{3,2,1,0:T(8,128)(2,1)S(1)} %reshape.48, f32[1024]{0:T(1024)S(1)} %bitcast.102, f32[1024]{0:T(1024)S(1)} %bitcast.101, f32[1024]{0:T(1024)S(1)} %bitcast.100, f32[1024]{0:T(1024)S(1)} %bitcast.99, f32[1024]{0:T(1024)S(1)} %bitcast.98, f32[1024]{0:T(1024)S(1)} %bitcast.97, ...), kind=kLoop, calls=%fused_computation.26 | loop fusion | flops 12582912 | bytes 8978432 | tf_op jit(solution)/shard_map/convert_element_type | solution.py:50
  128.6 4.8 %fusion.1 = f32[256,2048]{1,0:T(8,128)S(1)} fusion(bf16[256,1024]{1,0:T(8,128)(2,1)S(1)} %reshape.49, f32[1024,1024]{1,0:T(8,128)} %get-tuple-element.61, f32[1024,1024]{1,0:T(8,128)} %get-tuple-element.62), kind=kOutput, calls=%fused_computation.10 | convolution fusion | flops 1082130432 | bytes 11010048 | tf_op jit(solution)/shard_map/dot_general | solution.py:63
  135.8 2.8 %reshape.50 = f32[2,32,4,2,1024]{4,3,2,1,0:T(2,128)} reshape(f32[256,2048]{1,0:T(8,128)S(1)} %fusion.10) | data formatting | bytes 4194304 | tf_op jit(solution)/shard_map/reshape | solution.py:65
  138.6 5.4 %fusion.17 = (f32[1,32,4,1,1024]{4,3,2,1,0:T(1,128)S(1)}, f32[1,32,4,1,1024]{4,3,2,1,0:T(1,128)S(1)}, f32[1,32,4,1,1024]{4,3,2,1,0:T(1,128)}, f32[1,32,4,1,1024]{4,3,2,1,0:T(1,128)}) fusion(f32[2,32,4,2,1024]{4,3,2,1,0:T(2,128)} %reshape.50), kind=kLoop, calls=%fused_computation.44 | loop fusion | bytes 4194304 | tf_op jit(solution)/shard_map/slice | solution.py:67
  144.0 2.7 %copy.58 = f32[1,32,4,1,1024]{1,2,4,3,0:T(4,128)S(1)} copy(f32[1,32,4,1,1024]{4,3,2,1,0:T(1,128)} %get-tuple-element.40) | data formatting | bytes 1048576
  146.7 3.3 %copy.59 = f32[1,32,4,1,1024]{1,2,4,3,0:T(4,128)} copy(f32[1,32,4,1,1024]{4,3,2,1,0:T(1,128)} %get-tuple-element.39) | data formatting | bytes 1048576
  150.1 2.4 copy.60
  152.5 2.4 copy.61
  154.9 5.7 %add_reduce_fusion = (f32[32,1024]{0,1:T(8,128)S(1)}, bf16[32,4,1024]{0,1,2:T(4,128)(2,1)}, bf16[32,4,1024]{0,1,2:T(4,128)(2,1)}) fusion(f32[1,32,4,1,1024]{1,2,4,3,0:T(4,128)S(1)} %copy.58, f32[1,32,4,1,1024]{1,2,4,3,0:T(4,128)} %copy.59, f32[1,32,4,1,1024]{1,2,4,3,0:T(4,128)} %copy.60, f32[1,32,4,1,1024]{1,2,4,3,0:T(4,128)} %copy.61), kind=kLoop, calls=%fused_computation.21 | loop fusion | flops 1015808 | bytes 2752512 | tf_op jit(solution)/shard_map/reduce_sum | solution.py:86
  164.9 3.4 %all-to-all-start = ((bf16[4,2,512]{2,1,0:T(2,128)(2,1)}), bf16[4,2,512]{2,1,0:T(2,128)(2,1)S(1)}, u32[]{:S(2)}, u32[]{:S(2)}) async-start(bf16[4,2,512]{2,1,0:T(2,128)(2,1)} %reshape.92), calls=%async_computation | async-start | bytes 16384 | tf_op jit(solution)/shard_map/all_to_all | solution.py:93
  169.1 4.5 %all-to-all-done = bf16[4,2,512]{2,1,0:T(2,128)(2,1)S(1)} async-done(((bf16[4,2,512]{2,1,0:T(2,128)(2,1)}), bf16[4,2,512]{2,1,0:T(2,128)(2,1)S(1)}, u32[]{:S(2)}, u32[]{:S(2)}) %all-to-all-start) | async-done | bytes 8224 | tf_op jit(solution)/shard_map/all_to_all | solution.py:93
  173.9 8.0 %all_gather.9 = bf16[2,2,4,4,128]{4,3,2,1,0:T(4,128)(2,1)S(1)} all-gather(bf16[1,2,4,4,128]{4,3,2,1,0:T(4,128)(2,1)S(1)} %broadcast_in_dim.14), channel_id=1, replica_groups=mesh['elem_0'=8,'elem_1'=2,'elem_2'=8,'chan'=4] {'elem_1'}, dimensions={0}, use_global_device_ids=true | all-gather | bytes 24576 | tf_op jit(solution)/shard_map/all_gather | solution.py:23
  181.9 29.3 %all_gather.10 = bf16[16,2,4,4,128]{4,3,2,1,0:T(4,128)(2,1)} all-gather(bf16[2,2,4,4,128]{4,3,2,1,0:T(4,128)(2,1)S(1)} %all_gather.9), channel_id=1, replica_groups=mesh['elem_0'=8,'elem_1'=2,'elem_2'=8,'chan'=4] {'elem_0'}, dimensions={0}, use_global_device_ids=true | all-gather | bytes 147456 | tf_op jit(solution)/shard_map/all_gather | solution.py:23
  212.7 36.1 %all-gather.2.cloned.1.call-done = bf16[128,2,4,4,128]{4,3,2,1,0:T(4,128)(2,1)} async-done(((bf16[16,2,4,4,128]{4,3,2,1,0:T(4,128)(2,1)}), bf16[128,2,4,4,128]{4,3,2,1,0:T(4,128)(2,1)}) %all-gather.2.cloned.1.call-update) | async-done | bytes 1048592 | tf_op jit(solution)/shard_map/all_gather | solution.py:23
  (137 shorter events, 94.6 us)
Async XLA Ops:
  7.2 17.8 %copy-start.3 = (bf16[16,1024]{1,0:T(8,128)(2,1)S(1)}, bf16[16,1024]{1,0:T(8,128)(2,1)}, u32[]{:S(2)}) copy-start(bf16[16,1024]{1,0:T(8,128)(2,1)} %param.7) | copy-start | bytes 98308
  7.2 17.9 %copy-start.2 = (bf16[2,32,19584]{2,1,0:T(8,128)(2,1)S(1)}, bf16[2,32,19584]{2,1,0:T(8,128)(2,1)}, u32[]{:S(2)}) copy-start(bf16[2,32,19584]{2,1,0:T(8,128)(2,1)} %param.5) | copy-start | bytes 7520260
  25.0 2.0 copy-start.4
  128.6 4.9 %copy-start = (f32[1024,1024]{1,0:T(8,128)S(1)}, f32[1024,1024]{1,0:T(8,128)}, u32[]{:S(2)}) copy-start(f32[1024,1024]{1,0:T(8,128)} %get-tuple-element.61) | copy-start | bytes 12582916
  128.6 5.9 %copy-start.1 = (f32[1024,1024]{1,0:T(8,128)S(1)}, f32[1024,1024]{1,0:T(8,128)}, u32[]{:S(2)}) copy-start(f32[1024,1024]{1,0:T(8,128)} %get-tuple-element.62) | copy-start | bytes 12582916
  146.7 8.2 %copy-start.5 = (s32[16]{0:T(128)S(1)}, s32[16]{0:T(128)}, u32[]{:S(2)}) copy-start(s32[16]{0:T(128)} %param.8) | copy-start | bytes 196
  164.9 8.7 %all-to-all-start = ((bf16[4,2,512]{2,1,0:T(2,128)(2,1)}), bf16[4,2,512]{2,1,0:T(2,128)(2,1)S(1)}, u32[]{:S(2)}, u32[]{:S(2)}) async-start(bf16[4,2,512]{2,1,0:T(2,128)(2,1)} %reshape.92), calls=%async_computation | async-start | bytes 16384 | tf_op jit(solution)/shard_map/all_to_all | solution.py:93
  168.3 80.5 %all-gather.2.cloned.1.call-start = ((), (), s32[]{:S(2)}) async-start(), calls=%async_computation.1 | async-start | bytes 1179648 | tf_op jit(solution)/shard_map/all_gather | solution.py:23
Sparse Core Ops, SparseCore 0:
  211.3 37.5 all-gather.1
where the time goes:
time: 263 us; the launch traced here: 262 us
  local copies, waits for them, and re-layouts  128 us (49%)
  waiting for transfers between devices  40.6 us (15%)
  blocking collectives  37.3 us (14%)
  other arithmetic  29.3 us (11%)
  between operations  14.3 us (5%)
  matrix products  9.47 us (4%)
  starting transfers between devices  3.4 us (1%)
    gather x96, local copies, waits for them, and re-layouts  88.2 us
    all_gather x2, blocking collectives, all_blocks(): parts = lax.all_gather(parts, axes[k], axis=0, tiled=True)  37.3 us
    all_gather x1, waiting for transfers between devices, all_blocks(): parts = lax.all_gather(parts, axes[k], axis=0, tiled=True)  36.1 us
    mul x1, other arithmetic, spectra(): jnp.sin(radians) * factor  17.8 us
    unnamed x21, local copies, waits for them, and re-layouts  15.4 us
    reduce_sum x1, other arithmetic, on_device(): jnp.mean(spec_real * spec_real + spec_imag * spec_imag, axis=1)  5.69 us
    slice x1, local copies, waits for them, and re-layouts, spectra(): spec_imag = product[1, :, :, 0] - product[0, :, :, 1]  5.37 us
  transfers between devices with their start and end apart: 2, of which 2 were waited for; matrix products, arithmetic and copies ran while one was open for 1% of the time, Pallas kernels for 0%

commit v1 on v0

--- a/solution.py
+++ b/solution.py
@@ -20,7 +20,9 @@
 def all_blocks(array, axes, turns):
     parts = array[None]
     for k in turns:
-        parts = lax.all_gather(parts, axes[k], axis=0, tiled=True)
+        parts = jnp.concatenate(
+            lax.all_to_all(jnp.stack([parts] * lax.axis_size(axes[k])), axes[k], 0, 0), axis=0
+        )
     held = [lax.axis_size(axes[k]) for k in reversed(turns)]
     parts = parts.reshape(*held, *array.shape)
     turned = sorted(range(len(turns)), key=lambda place: turns[len(turns) - 1 - place])

time: 263 us -> 235 us (0.89)
  the two profiles are of different devices: /device:TPU:2 before, /device:TPU:8 now
where the time goes in v1:
time: 235 us; the launch traced here: 233 us
  local copies, waits for them, and re-layouts  127 us (54%)
  waiting for transfers between devices  32.7 us (14%)
  other arithmetic  29.3 us (12%)
  starting transfers between devices  17.9 us (8%)
  blocking collectives  15.6 us (7%)
  matrix products  9.47 us (4%)
    gather x96, local copies, waits for them, and re-layouts  88.2 us
    all_to_all x2, waiting for transfers between devices, all_blocks(): lax.all_to_all(jnp.stack([parts] * lax.axis_size(axes[k])), axes[k], 0, 0)  32.7 us
    all_to_all x2, starting transfers between devices, all_blocks(): lax.all_to_all(jnp.stack([parts] * lax.axis_size(axes[k])), axes[k], 0, 0)  17.9 us
    mul x1, other arithmetic, spectra(): jnp.sin(radians) * factor  17.8 us
    unnamed x23, local copies, waits for them, and re-layouts  14.8 us
    all_to_all x1, blocking collectives, on_device(): lax.all_to_all(picked, 'chan', split_axis=1, concat_axis=3, tiled=True)  9.41 us
    all_to_all x1, blocking collectives, all_blocks(): lax.all_to_all(jnp.stack([parts] * lax.axis_size(axes[k])), axes[k], 0, 0)  6.2 us
    reduce_sum x1, other arithmetic, on_device(): jnp.mean(spec_real * spec_real + spec_imag * spec_imag, axis=1)  5.69 us
  transfers between devices with their start and end apart: 2, of which 2 were waited for; matrix products, arithmetic and copies ran while one was open for 0% of the time, Pallas kernels for 0%

profile of v1, /device:TPU:8, one launch (start us, length us, event | category | flops | bytes accessed | tf_op | source)
XLA Modules:
  0.0 233.3 jit_solution(12180305149648651257)
XLA Ops:
  0.7 17.8 %sine_multiply_fusion = (f32[1024,1024]{1,0:T(8,128)}, f32[1024,1024]{1,0:T(8,128)}) fusion(), kind=kLoop, calls=%fused_computation.14 | loop fusion | flops 16777216 | bytes 8388608 | tf_op jit(solution)/shard_map/mul | solution.py:61
  20.6 88.3 %while.1 = (s32[]{:T(128)}, bf16[2,32,19584]{2,0,1:T(2,128)(2,1)S(1)}, s32[32,2]{0,1:T(2,128)S(1)}, bf16[32,2,19456]{2,1,0:T(2,128)(2,1)}, s32[]{:T(128)}) while((s32[]{:T(128)}, bf16[2,32,19584]{2,0,1:T(2,128)(2,1)S(1)}, s32[32,2]{0,1:T(2,128)S(1)}, bf16[32,2,19456]{2,1,0:T(2,128)(2,1)}, s32[]{:T(128)}) %tuple.52), condition=%wide.while_cond, body=%wide.while_body.sunk | while | flops 2 | bytes 157281 | solution.py:42
  32.2 2.1 bitcast_dynamic-update-slice_fusion.2
  37.7 2.1 bitcast_dynamic-update-slice_fusion.2
  40.5 2.1 bitcast_dynamic-update-slice_fusion.2
  81.9 2.1 bitcast_dynamic-update-slice_fusion.2
  106.7 2.1 bitcast_dynamic-update-slice_fusion.2
  108.8 3.6 %copy.43 = bf16[2,32,19456]{2,1,0:T(8,128)(2,1)} copy(bf16[2,32,19456]{2,0,1:T(2,128)(2,1)} %bitcast.84) | data formatting | bytes 4980736 | tf_op jit(solution)/shard_map/vmap(vmap())/gather | solution.py:42
  112.5 3.3 %reshape.49 = bf16[2,32,19,1024]{3,2,1,0:T(8,128)(2,1)S(1)} reshape(bf16[2,32,19456]{2,1,0:T(8,128)(2,1)} %copy.43) | data formatting | bytes 4980736 | tf_op jit(solution)/shard_map/reshape | solution.py:45
  115.8 5.1 %add_convert_fusion = bf16[2,32,4,1024]{3,2,1,0:T(4,128)(2,1)} fusion(bf16[2,32,19,1024]{3,2,1,0:T(8,128)(2,1)S(1)} %reshape.49, f32[1024]{0:T(1024)S(1)} %bitcast.106, f32[1024]{0:T(1024)S(1)} %bitcast.105, f32[1024]{0:T(1024)S(1)} %bitcast.104, f32[1024]{0:T(1024)S(1)} %bitcast.103, f32[1024]{0:T(1024)S(1)} %bitcast.102, f32[1024]{0:T(1024)S(1)} %bitcast.101, ...), kind=kLoop, calls=%fused_computation.26 | loop fusion | flops 12582912 | bytes 8978432 | tf_op jit(solution)/shard_map/convert_element_type | solution.py:52
  122.1 4.8 %fusion.1 = f32[256,2048]{1,0:T(8,128)S(1)} fusion(bf16[256,1024]{1,0:T(8,128)(2,1)S(1)} %reshape.50, f32[1024,1024]{1,0:T(8,128)} %get-tuple-element.63, f32[1024,1024]{1,0:T(8,128)} %get-tuple-element.64), kind=kOutput, calls=%fused_computation.10 | convolution fusion | flops 1082130432 | bytes 11010048 | tf_op jit(solution)/shard_map/dot_general | solution.py:65
  129.3 2.8 %reshape.51 = f32[2,32,4,2,1024]{4,3,2,1,0:T(2,128)} reshape(f32[256,2048]{1,0:T(8,128)S(1)} %fusion.10) | data formatting | bytes 4194304 | tf_op jit(solution)/shard_map/reshape | solution.py:67
  132.1 5.4 %fusion.17 = (f32[1,32,4,1,1024]{4,3,2,1,0:T(1,128)S(1)}, f32[1,32,4,1,1024]{4,3,2,1,0:T(1,128)S(1)}, f32[1,32,4,1,1024]{4,3,2,1,0:T(1,128)}, f32[1,32,4,1,1024]{4,3,2,1,0:T(1,128)}) fusion(f32[2,32,4,2,1024]{4,3,2,1,0:T(2,128)} %reshape.51), kind=kLoop, calls=%fused_computation.45 | loop fusion | bytes 4194304 | tf_op jit(solution)/shard_map/slice | solution.py:69
  137.5 2.7 %copy.61 = f32[1,32,4,1,1024]{1,2,4,3,0:T(4,128)S(1)} copy(f32[1,32,4,1,1024]{4,3,2,1,0:T(1,128)} %get-tuple-element.42) | data formatting | bytes 1048576
  140.2 3.3 %copy.62 = f32[1,32,4,1,1024]{1,2,4,3,0:T(4,128)} copy(f32[1,32,4,1,1024]{4,3,2,1,0:T(1,128)} %get-tuple-element.41) | data formatting | bytes 1048576
  143.5 2.4 %copy.63 = f32[1,32,4,1,1024]{1,2,4,3,0:T(4,128)} copy(f32[1,32,4,1,1024]{4,3,2,1,0:T(1,128)S(1)} %get-tuple-element.40) | data formatting | bytes 1048576
  145.9 2.4 %copy.64 = f32[1,32,4,1,1024]{1,2,4,3,0:T(4,128)} copy(f32[1,32,4,1,1024]{4,3,2,1,0:T(1,128)S(1)} %get-tuple-element.39) | data formatting | bytes 1048576
  148.4 5.7 %add_reduce_fusion = (f32[32,1024]{0,1:T(8,128)S(1)}, bf16[32,4,1024]{0,1,2:T(4,128)(2,1)}, bf16[32,4,1024]{0,1,2:T(4,128)(2,1)}) fusion(f32[1,32,4,1,1024]{1,2,4,3,0:T(4,128)S(1)} %copy.61, f32[1,32,4,1,1024]{1,2,4,3,0:T(4,128)} %copy.62, f32[1,32,4,1,1024]{1,2,4,3,0:T(4,128)} %copy.63, f32[1,32,4,1,1024]{1,2,4,3,0:T(4,128)} %copy.64), kind=kLoop, calls=%fused_computation.21 | loop fusion | flops 1015808 | bytes 2752512 | tf_op jit(solution)/shard_map/reduce_sum | solution.py:88
  157.9 9.4 %all_to_all.30 = bf16[4,2,512]{2,1,0:T(2,128)(2,1)S(1)} all-to-all(bf16[4,2,512]{2,1,0:T(2,128)(2,1)S(1)} %reshape.92), channel_id=1, replica_groups=mesh['elem_0'=8,'elem_1'=2,'elem_2'=8,'chan'=4] {'chan'}, dimensions={0} | all-to-all | bytes 16384 | tf_op jit(solution)/shard_map/all_to_all | solution.py:95
  167.6 6.2 %all_to_all.31 = bf16[2,1,2,4,4,128]{5,4,3,2,1,0:T(4,128)(2,1)S(1)} all-to-all(bf16[2,1,2,4,4,128]{5,4,3,2,1,0:T(4,128)(2,1)S(1)} %pad_maximum_fusion.1), channel_id=1, replica_groups=mesh['elem_0'=8,'elem_1'=2,'elem_2'=8,'chan'=4] {'elem_1'}, dimensions={0} | all-to-all | bytes 32768 | tf_op jit(solution)/shard_map/all_to_all | solution.py:24
  174.5 10.3 %all-to-all-start.2 = ((bf16[8,2,2,4,4,128]{5,1,4,3,2,0:T(2,128)(2,1)}), bf16[8,2,2,4,4,128]{5,1,4,3,2,0:T(2,128)(2,1)S(1)}, u32[]{:S(2)}, u32[]{:S(2)}) async-start(bf16[8,2,2,4,4,128]{5,1,4,3,2,0:T(2,128)(2,1)} %stack.34), calls=%async_computation.2 | async-start | bytes 262144 | tf_op jit(solution)/shard_map/all_to_all | solution.py:24
  185.6 8.3 %all-to-all-done.2 = bf16[8,2,2,4,4,128]{5,1,4,3,2,0:T(2,128)(2,1)S(1)} async-done(((bf16[8,2,2,4,4,128]{5,1,4,3,2,0:T(2,128)(2,1)}), bf16[8,2,2,4,4,128]{5,1,4,3,2,0:T(2,128)(2,1)S(1)}, u32[]{:S(2)}, u32[]{:S(2)}) %all-to-all-start.2) | async-done | bytes 131104 | tf_op jit(solution)/shard_map/all_to_all | solution.py:24
  195.2 7.5 %all-to-all-start.3 = ((bf16[8,16,2,4,4,128]{5,1,4,3,2,0:T(8,128)(2,1)}), bf16[8,16,2,4,4,128]{5,1,4,3,2,0:T(8,128)(2,1)S(1)}, u32[]{:S(2)}, u32[]{:S(2)}) async-start(bf16[8,16,2,4,4,128]{5,1,4,3,2,0:T(8,128)(2,1)} %stack.35), calls=%async_computation.3 | async-start | bytes 2097152 | tf_op jit(solution)/shard_map/all_to_all | solution.py:24
  203.1 24.4 %all-to-all-done.3 = bf16[8,16,2,4,4,128]{5,1,4,3,2,0:T(8,128)(2,1)S(1)} async-done(((bf16[8,16,2,4,4,128]{5,1,4,3,2,0:T(8,128)(2,1)}), bf16[8,16,2,4,4,128]{5,1,4,3,2,0:T(8,128)(2,1)S(1)}, u32[]{:S(2)}, u32[]{:S(2)}) %all-to-all-start.3) | async-done | bytes 1048608 | tf_op jit(solution)/shard_map/all_to_all | solution.py:24
  (142 shorter events, 96.2 us)
Async XLA Ops:
  0.6 17.8 %copy-start.4 = (bf16[16,1024]{1,0:T(8,128)(2,1)S(1)}, bf16[16,1024]{1,0:T(8,128)(2,1)}, u32[]{:S(2)}) copy-start(bf16[16,1024]{1,0:T(8,128)(2,1)} %param.7) | copy-start | bytes 98308
  0.7 17.9 %copy-start.2 = (bf16[2,32,19584]{2,1,0:T(8,128)(2,1)S(1)}, bf16[2,32,19584]{2,1,0:T(8,128)(2,1)}, u32[]{:S(2)}) copy-start(bf16[2,32,19584]{2,1,0:T(8,128)(2,1)} %param.5) | copy-start | bytes 7520260
  18.5 2.0 copy-start.5
  122.0 4.9 %copy-start = (f32[1024,1024]{1,0:T(8,128)S(1)}, f32[1024,1024]{1,0:T(8,128)}, u32[]{:S(2)}) copy-start(f32[1024,1024]{1,0:T(8,128)} %get-tuple-element.63) | copy-start | bytes 12582916
  122.0 5.9 %copy-start.1 = (f32[1024,1024]{1,0:T(8,128)S(1)}, f32[1024,1024]{1,0:T(8,128)}, u32[]{:S(2)}) copy-start(f32[1024,1024]{1,0:T(8,128)} %get-tuple-element.64) | copy-start | bytes 12582916
  140.2 8.2 %copy-start.6 = (s32[16]{0:T(128)S(1)}, s32[16]{0:T(128)}, u32[]{:S(2)}) copy-start(s32[16]{0:T(128)} %param.8) | copy-start | bytes 196
  154.1 48.7 %copy-start.3 = (bf16[4,2,4,16384]{3,2,1,0:T(4,128)(2,1)S(1)}, bf16[4,2,4,16384]{3,2,1,0:T(4,128)(2,1)}, u32[]{:S(2)}) copy-start(bf16[4,2,4,16384]{3,2,1,0:T(4,128)(2,1)} %param.9) | copy-start | bytes 3145732
  174.5 19.4 %all-to-all-start.2 = ((bf16[8,2,2,4,4,128]{5,1,4,3,2,0:T(2,128)(2,1)}), bf16[8,2,2,4,4,128]{5,1,4,3,2,0:T(2,128)(2,1)S(1)}, u32[]{:S(2)}, u32[]{:S(2)}) async-start(bf16[8,2,2,4,4,128]{5,1,4,3,2,0:T(2,128)(2,1)} %stack.34), calls=%async_computation.2 | async-start | bytes 262144 | tf_op jit(solution)/shard_map/all_to_all | solution.py:24
  195.2 32.3 %all-to-all-start.3 = ((bf16[8,16,2,4,4,128]{5,1,4,3,2,0:T(8,128)(2,1)}), bf16[8,16,2,4,4,128]{5,1,4,3,2,0:T(8,128)(2,1)S(1)}, u32[]{:S(2)}, u32[]{:S(2)}) async-start(bf16[8,16,2,4,4,128]{5,1,4,3,2,0:T(8,128)(2,1)} %stack.35), calls=%async_computation.3 | async-start | bytes 2097152 | tf_op jit(solution)/shard_map/all_to_all | solution.py:24
